TPU v7x, 32 devices: a whole 2x2x4 slice. The times are simulated.
32 devices in a mesh: tm: 4 (over y, x), users: 8 (over z, core).
Axes of the slice: x: 2, y: 2, z: 4, core: 2. Of those that a mesh axis runs over, the one named last changes fastest.
Arguments:
- features: float32 [131072, 128], P(('tm', 'users')), may hold values from -6 to 6
- home: int32 [131072, 1], P(('tm', 'users')), may hold values from 0 to 7; in each aligned block of 4096 rows (0 to 4095, 4096 to 8191, ...) at most 1024 rows name the same one
- account: int32 [131072], P(('tm', 'users')), may hold values from 0 to 127
- flags: int32 [131072], P(('tm', 'users')), may hold values 0 or 1
Outputs:
- session_mean: float32 [131072, 128], P(('tm', 'users'))
Inputs may be any that keep to these rules, and one draw needn't show every extreme that they name: `home`: the 4096 events of one device name one owner at most 1024 times, a bound that some block reaches.
All inputs are finite; a program needn't handle non-finite values. No bound on the sum of `flags` on one device may be relied on, other than what follows from the above.
Results may differ from a plain program's by a relative error of at most 0.00007.
Values sent between devices are 32-bit elements; how exact they have to be, the bound alone decides.
No kernel may reach another device: no remote copies, remote signals or barrier semaphores. Data moves between devices by JAX's collectives and lax.ppermute only.
A program may use at most 64 MiB of HBM per device.

v0:
```python
import math
import jax
import jax.numpy as jnp
from jax import lax
from jax.sharding import PartitionSpec as P

ACCOUNTS = 128
EXACT_MATMUL = lax.Precision.HIGHEST


def destination_rank(owner_of, owners):
    count_per_row = owner_of.shape[0]
    block_rows = math.gcd(count_per_row, 512)
    blocks = count_per_row // block_rows
    strict_lower = (
        lax.broadcasted_iota(jnp.int32, (block_rows, block_rows), 0)
        > lax.broadcasted_iota(jnp.int32, (block_rows, block_rows), 1)
    ).astype(jnp.float32)
    columns = jnp.arange(owners, dtype=jnp.int32)

    def destination_advance(before, block_data):
        choose_mask = (block_data[:, None] == columns[None, :]).astype(jnp.float32)
        earlier = jnp.dot(strict_lower, choose_mask, precision=EXACT_MATMUL) + before[None, :]
        return (before + jnp.sum(choose_mask, axis=0), jnp.sum(earlier * choose_mask, axis=1))

    ignored, rank_rows = lax.scan(
        destination_advance, jnp.zeros((owners,), jnp.float32), owner_of.reshape(blocks, block_rows)
    )
    return rank_rows.reshape(count_per_row).astype(jnp.int32)


def decode_rows(code_rows):
    code_ints = code_rows.astype(jnp.int32)
    is_valid = code_ints >= 0
    account_rows = jnp.where(is_valid, code_ints // 2, -1)
    flag_rows = jnp.where(is_valid, code_ints % 2, 0).astype(jnp.float32)
    return (account_rows, flag_rows)


def session_sweep(values, account_rows, flag_rows, accounts):
    count_per_row, feature_count = values.shape
    block_rows = math.gcd(count_per_row, 512)
    blocks = count_per_row // block_rows
    row_ids = lax.broadcasted_iota(jnp.int32, (block_rows, block_rows), 0)
    col_ids = lax.broadcasted_iota(jnp.int32, (block_rows, block_rows), 1)
    up_to = col_ids <= row_ids
    later_rows = col_ids > row_ids
    up_to_float = up_to.astype(jnp.float32)
    columns = jnp.arange(accounts, dtype=jnp.int32)

    def session_advance(carried, block_data):
        open_sum, open_count, already_seen = carried
        rows_values, rows_account, rows_flag = block_data
        is_live = rows_account >= 0
        indicator_matrix = (rows_account[:, None] == columns[None, :]).astype(jnp.float32)
        flag_counts = jnp.dot(
            up_to_float, indicator_matrix * rows_flag[:, None], precision=EXACT_MATMUL
        )
        own_flags = jnp.sum(flag_counts * indicator_matrix, axis=1)
        same_user = (
            (rows_account[:, None] == rows_account[None, :]) & is_live[None, :] & is_live[:, None]
        )
        same_session = (same_user & up_to & (own_flags[:, None] == own_flags[None, :])).astype(
            jnp.float32
        )
        inside_sum = jnp.dot(same_session, rows_values, precision=EXACT_MATMUL)
        inside_count = jnp.sum(same_session, axis=1)
        session_continues = jnp.where(is_live & (own_flags == 0.0), 1.0, 0.0)
        running_sum = inside_sum + session_continues[:, None] * jnp.dot(
            indicator_matrix, open_sum, precision=EXACT_MATMUL
        )
        running_count = inside_count + session_continues * jnp.dot(
            indicator_matrix, open_count, precision=EXACT_MATMUL
        )
        without_flag = session_continues * (
            1.0 - jnp.dot(indicator_matrix, already_seen, precision=EXACT_MATMUL)
        )
        followers = jnp.sum((same_user & later_rows).astype(jnp.float32), axis=1)
        last_weight = jnp.where(is_live & (followers == 0.0), 1.0, 0.0)
        present = jnp.minimum(jnp.sum(indicator_matrix, axis=0), 1.0)
        updated_sum = (
            jnp.einsum(
                "ra,rf->af",
                indicator_matrix,
                last_weight[:, None] * running_sum,
                precision=EXACT_MATMUL,
            )
            + (1.0 - present)[:, None] * open_sum
        )
        updated_count = (
            jnp.dot(last_weight * running_count, indicator_matrix, precision=EXACT_MATMUL)
            + (1.0 - present) * open_count
        )
        any_flag = jnp.minimum(jnp.sum(indicator_matrix * rows_flag[:, None], axis=0), 1.0)
        updated_seen = jnp.maximum(already_seen, any_flag)
        return (
            (updated_sum, updated_count, updated_seen),
            (running_sum, running_count, without_flag),
        )

    start_state = (
        jnp.zeros((accounts, feature_count), jnp.float32),
        jnp.zeros((accounts,), jnp.float32),
        jnp.zeros((accounts,), jnp.float32),
    )
    block_data = (
        values.reshape(blocks, block_rows, feature_count),
        account_rows.reshape(blocks, block_rows),
        flag_rows.reshape(blocks, block_rows),
    )
    closing_state, row_pieces = lax.scan(session_advance, start_state, block_data)
    running_sum = row_pieces[0].reshape(count_per_row, feature_count)
    running_count = row_pieces[1].reshape(count_per_row)
    without_flag = row_pieces[2].reshape(count_per_row)
    return (closing_state, running_sum, running_count, without_flag)


def combine_states(earlier, later):
    carry_on = 1.0 - later[2]
    return (
        later[0] + carry_on[:, None] * earlier[0],
        later[1] + carry_on * earlier[1],
        jnp.maximum(earlier[2], later[2]),
    )


def body(features, home, account, flags):
    owners = lax.axis_size("users")
    event_rows, feature_count = features.shape
    slot_cap = 2 * event_rows // owners
    accounts = ACCOUNTS
    owner_of = home[:, 0]
    rank_rows = destination_rank(owner_of, owners)
    slot_index = owner_of * slot_cap + rank_rows
    code_values = (account * 2 + flags).astype(jnp.float32)
    send_values = (
        jnp.zeros((owners * slot_cap, feature_count), jnp.float32).at[slot_index].set(features)
    )
    send_codes = jnp.full((owners * slot_cap,), -1.0, jnp.float32).at[slot_index].set(code_values)
    got_values, got_codes = (
        lax.all_to_all(
            send_values.reshape(owners, slot_cap, feature_count),
            "users",
            split_axis=0,
            concat_axis=0,
            tiled=True,
        ),
        lax.all_to_all(
            send_codes.reshape(owners, slot_cap), "users", split_axis=0, concat_axis=0, tiled=True
        ),
    )
    account_rows, flag_rows = decode_rows(got_codes.reshape(owners * slot_cap))
    closing_state, running_sum, running_count, without_flag = session_sweep(
        got_values.reshape(owners * slot_cap, feature_count), account_rows, flag_rows, accounts
    )
    identity = (
        jnp.zeros((accounts, feature_count), jnp.float32),
        jnp.zeros((accounts,), jnp.float32),
        jnp.zeros((accounts,), jnp.float32),
    )
    gathered = (
        lax.all_gather(closing_state[0], "tm", axis=0, tiled=True),
        lax.all_gather(closing_state[1], "tm", axis=0, tiled=True),
        lax.all_gather(closing_state[2], "tm", axis=0, tiled=True),
    )
    my_group = lax.axis_index("tm")
    incoming = identity
    for position in range(lax.axis_size("tm")):
        group_state = (
            gathered[0][position * accounts : (position + 1) * accounts],
            gathered[1][position * accounts : (position + 1) * accounts],
            gathered[2][position * accounts : (position + 1) * accounts],
        )
        merged = combine_states(incoming, group_state)
        incoming = (
            jnp.where(position < my_group, merged[0], incoming[0]),
            jnp.where(position < my_group, merged[1], incoming[1]),
            jnp.where(position < my_group, merged[2], incoming[2]),
        )
    columns = jnp.arange(accounts, dtype=jnp.int32)
    onehot_rows = (account_rows[:, None] == columns[None, :]).astype(jnp.float32)
    overall_sum = running_sum + without_flag[:, None] * jnp.dot(
        onehot_rows, incoming[0], precision=EXACT_MATMUL
    )
    overall_count = running_count + without_flag * jnp.dot(
        onehot_rows, incoming[1], precision=EXACT_MATMUL
    )
    session_means = overall_sum / jnp.where(overall_count > 0.0, overall_count, 1.0)[:, None]
    returned_means = lax.all_to_all(
        session_means.reshape(owners, slot_cap, feature_count),
        "users",
        split_axis=0,
        concat_axis=0,
        tiled=True,
    )
    result = returned_means.reshape(owners * slot_cap, feature_count)[slot_index]
    return result


def solution(mesh):
    return jax.shard_map(
        body,
        mesh=mesh,
        in_specs=(
            P(("tm", "users"), None),
            P(("tm", "users"), None),
            P(("tm", "users")),
            P(("tm", "users")),
        ),
        out_specs=P(("tm", "users"), None),
        check_vma=False,
    )
```

profile of v0, /device:TPU:0, one launch (start us, length us, event | category | flops | bytes accessed | tf_op | source)
XLA Modules:
  0.0 385.4 jit_solution(16359685620664613377)
XLA Ops:
  0.6 1.4 reduce.7
  2.1 5.3 %while.34 = (s32[]{:T(128)}, f32[8]{0:T(128)S(1)}, f32[8,512]{1,0:T(8,128)S(1)}, s32[8,512]{1,0:T(8,128)S(1)}, s32[]{:T(128)}, /*index=5*/s32[]{:T(128)}) while((s32[]{:T(128)}, f32[8]{0:T(128)S(1)}, f32[8,512]{1,0:T(8,128)S(1)}, s32[8,512]{1,0:T(8,128)S(1)}, s32[]{:T(128)}, /*index=5*/s32[]{:T(128)}) %tuple.69), condition=%wide.region_3.4_spmd.clone, body=%wide.region_0.3_spmd.clone.sunk | while | flops 25722380 | bytes 14623 | solution.py:26
  8.9 16.1 %scatter_custom_fusion = f32[8192]{0:T(1024)} fusion(s32[4096]{0:T(1024)S(1)} %bitcast.173, f32[4096]{0:T(1024)S(1)} %add_convert_fusion, f32[]{:T(128)} %constant.54.clone.1), kind=kCustom, calls=%fused_computation.134 | custom fusion | bytes 32772 | tf_op jit(solution)/shard_map/scatter | solution.py:139
  25.0 6.4 %all-to-all-start = ((f32[8,1,1024]{2,1,0:T(1,128)}), f32[8,1,1024]{2,1,0:T(1,128)S(1)}, u32[]{:S(2)}, u32[]{:S(2)}) async-start(f32[8,1,1024]{2,1,0:T(1,128)} %bitcast.1), calls=%async_computation | async-start | bytes 65536 | tf_op jit(solution)/shard_map/all_to_all | solution.py:148
  31.3 13.1 %scatter_custom_fusion.1 = f32[8192,128]{1,0:T(8,128)} fusion(s32[4096]{0:T(1024)S(1)} %bitcast.174, f32[4096,128]{1,0:T(8,128)} %param.8, f32[]{:T(128)} %constant.49.clone.1), kind=kCustom, calls=%fused_computation.88 | custom fusion | bytes 4194816 | tf_op jit(solution)/shard_map/scatter | solution.py:137
  44.4 5.1 %all-to-all-start.1 = ((f32[8,1024,128]{2,1,0:T(8,128)}), f32[8,1024,128]{2,1,0:T(8,128)}, u32[]{:S(2)}, u32[]{:S(2)}) async-start(f32[8,1024,128]{2,1,0:T(8,128)} %bitcast.151), calls=%async_computation.1 | async-start | bytes 8388608 | tf_op jit(solution)/shard_map/all_to_all | solution.py:141
  49.8 93.8 %all-to-all-done.1 = f32[8,1024,128]{2,1,0:T(8,128)} async-done(((f32[8,1024,128]{2,1,0:T(8,128)}), f32[8,1024,128]{2,1,0:T(8,128)}, u32[]{:S(2)}, u32[]{:S(2)}) %all-to-all-start.1) | async-done | bytes 4194336 | tf_op jit(solution)/shard_map/all_to_all | solution.py:141
  143.6 90.4 %while.35 = (s32[]{:T(128)}, f32[128,128]{1,0:T(8,128)S(1)}, f32[128]{0:T(128)S(1)}, f32[128]{0:T(128)S(1)}, f32[16,512,128]{2,1,0:T(8,128)}, /*index=5*/f32[16,...) while((s32[]{:T(128)}, f32[128,128]{1,0:T(8,128)S(1)}, ...), condition=%wide.region_12.13_spmd.clone, body=%wide.region_6.12_spmd.clone.sunk | while | flops 1016011008 | bytes 1867940 | solution.py:111
  146.0 1.7 fusion.150
  147.7 1.1 bitcast_dynamic-update-slice_fusion.2
  151.6 1.7 fusion.150
  153.3 1.1 bitcast_dynamic-update-slice_fusion.2
  157.3 1.7 fusion.150
  159.0 1.1 bitcast_dynamic-update-slice_fusion.2
  162.9 1.7 fusion.150
  164.6 1.1 bitcast_dynamic-update-slice_fusion.2
  168.6 1.7 fusion.150
  170.3 1.1 bitcast_dynamic-update-slice_fusion.2
  174.2 1.7 fusion.150
  176.0 1.1 bitcast_dynamic-update-slice_fusion.2
  179.9 1.7 fusion.150
  181.6 1.1 bitcast_dynamic-update-slice_fusion.2
  185.6 1.7 fusion.150
  187.3 1.1 bitcast_dynamic-update-slice_fusion.2
  191.2 1.7 fusion.150
  192.9 1.1 bitcast_dynamic-update-slice_fusion.2
  196.9 1.7 fusion.150
  198.6 1.1 bitcast_dynamic-update-slice_fusion.2
  202.5 1.7 fusion.150
  204.2 1.1 bitcast_dynamic-update-slice_fusion.2
  208.2 1.7 fusion.150
  209.9 1.1 bitcast_dynamic-update-slice_fusion.2
  213.8 1.7 fusion.150
  215.5 1.1 bitcast_dynamic-update-slice_fusion.2
  219.5 1.7 fusion.150
  221.2 1.1 bitcast_dynamic-update-slice_fusion.2
  225.1 1.7 fusion.150
  226.8 1.1 bitcast_dynamic-update-slice_fusion.2
  230.8 1.7 fusion.150
  232.5 1.1 bitcast_dynamic-update-slice_fusion.2
  234.0 8.0 %all-gather = f32[4,1,128]{2,1,0:T(1,128)S(1)} all-gather(f32[1,1,128]{2,1,0:T(1,128)S(1)} %bitcast.184), channel_id=1, replica_groups=mesh['tm'=4,'users'=8] {'tm'}, dimensions={0}, use_global_device_ids=true | all-gather | bytes 2560 | tf_op jit(solution)/shard_map/all_gather | solution.py:164
  242.0 7.9 %all-gather.1 = f32[4,1,128]{2,1,0:T(1,128)S(1)} all-gather(f32[1,1,128]{2,1,0:T(1,128)S(1)} %bitcast.185), channel_id=1, replica_groups=mesh['tm'=4,'users'=8] {'tm'}, dimensions={0}, use_global_device_ids=true | all-gather | bytes 2560 | tf_op jit(solution)/shard_map/all_gather | solution.py:163
  249.9 8.0 %all_gather.9 = f32[512,128]{1,0:T(8,128)S(1)} all-gather(f32[128,128]{1,0:T(8,128)S(1)} %get-tuple-element.117), channel_id=1, replica_groups=mesh['tm'=4,'users'=8] {'tm'}, dimensions={0}, use_global_device_ids=true | all-gather | bytes 327680 | tf_op jit(solution)/shard_map/all_gather | solution.py:162
  257.9 2.9 fusion.58
  260.9 9.6 %fusion.57 = f32[8192,128]{1,0:T(8,128)} fusion(f32[8192,128]{1,0:T(8,128)} %bitcast.186, f32[8192]{0:T(1024)S(1)} %compare_select_fusion.1, s32[8192]{0:T(1024)S(1)} %fusion.78, f32[8192]{0:T(1024)S(1)} %bitcast.171, f32[512,128]{1,0:T(8,128)S(1)} %all_gather.9, f32[128]{0:T(128)S(1)} %get-tuple-element.232, f32[128]{0:T(128)S(1)} %get-tuple-element.230, ...), kind=kOutput, calls=%fused_computation.83 | convolution fusion | flops 1614987264 | bytes 8751108 | tf_op jit(solution)/shard_map/dot_general | solution.py:182
  270.5 4.5 %all-to-all-start.2 = ((f32[8,1024,128]{2,1,0:T(8,128)}), f32[8,1024,128]{2,1,0:T(8,128)}, u32[]{:S(2)}, u32[]{:S(2)}) async-start(f32[8,1024,128]{2,1,0:T(8,128)} %bitcast.152), calls=%async_computation.2 | async-start | bytes 8388608 | tf_op jit(solution)/shard_map/all_to_all | solution.py:189
  275.1 94.0 %all-to-all-done.2 = f32[8,1024,128]{2,1,0:T(8,128)} async-done(((f32[8,1024,128]{2,1,0:T(8,128)}), f32[8,1024,128]{2,1,0:T(8,128)}, u32[]{:S(2)}, u32[]{:S(2)}) %all-to-all-start.2) | async-done | bytes 4194336 | tf_op jit(solution)/shard_map/all_to_all | solution.py:189
  369.0 16.4 %gather_fusion = f32[4096,128]{1,0:T(8,128)} fusion(f32[8192,128]{1,0:T(8,128)} %bitcast.19, s32[4096]{0:T(1024)S(1)} %broadcast_clamp_fusion), kind=kCustom, calls=%fused_computation | custom fusion | bytes 4210688 | tf_op jit(solution)/shard_map/gather | solution.py:196
  (289 shorter events, 51.4 us)
Async XLA Ops:
  25.0 19.5 %all-to-all-start = ((f32[8,1,1024]{2,1,0:T(1,128)}), f32[8,1,1024]{2,1,0:T(1,128)S(1)}, u32[]{:S(2)}, u32[]{:S(2)}) async-start(f32[8,1,1024]{2,1,0:T(1,128)} %bitcast.1), calls=%async_computation | async-start | bytes 65536 | tf_op jit(solution)/shard_map/all_to_all | solution.py:148
  44.4 99.2 %all-to-all-start.1 = ((f32[8,1024,128]{2,1,0:T(8,128)}), f32[8,1024,128]{2,1,0:T(8,128)}, u32[]{:S(2)}, u32[]{:S(2)}) async-start(f32[8,1024,128]{2,1,0:T(8,128)} %bitcast.151), calls=%async_computation.1 | async-start | bytes 8388608 | tf_op jit(solution)/shard_map/all_to_all | solution.py:141
  270.5 98.5 %all-to-all-start.2 = ((f32[8,1024,128]{2,1,0:T(8,128)}), f32[8,1024,128]{2,1,0:T(8,128)}, u32[]{:S(2)}, u32[]{:S(2)}) async-start(f32[8,1024,128]{2,1,0:T(8,128)} %bitcast.152), calls=%async_computation.2 | async-start | bytes 8388608 | tf_op jit(solution)/shard_map/all_to_all | solution.py:189
where the time goes:
time: 387 us; the launch traced here: 385 us
  waiting for transfers between devices  188 us (49%)
  matrix products  90.2 us (23%)
  local copies, waits for them, and re-layouts  49.7 us (13%)
  blocking collectives  23.9 us (6%)
  other arithmetic  16.1 us (4%)
  starting transfers between devices  16 us (4%)
    all_to_all x1, waiting for transfers between devices, body(): lax.all_to_all(session_means.reshape(owners, slot_cap, feature_count), 'u...  94 us
    all_to_all x1, waiting for transfers between devices, body(): lax.all_to_all(send_values.reshape(owners, slot_cap, feature_count), 'use...  93.8 us
    dot_general x16, matrix products, session_advance(): inside_sum = jnp.dot(same_session, rows_values, precision=EXACT_MATMUL)  27.3 us
    dot_general x16, matrix products, session_advance(): jnp.dot(indicator_matrix, open_sum, precision=EXACT_MATMUL)  17.8 us
    gather x1, local copies, waits for them, and re-layouts, body(): returned_means.reshape(owners * slot_cap, feature_count)[slot_index]  16.4 us
    scatter x1, local copies, waits for them, and re-layouts, body(): jnp.full((owners * slot_cap,), -1.0, jnp.float32).at[slot_index]  16.1 us
    dot_general x16, matrix products, session_advance(): jnp.dot(up_to_float, indicator_matrix * rows_flag[:, None], precision=EXA...  14.1 us
    scatter x1, local copies, waits for them, and re-layouts, body(): jnp.zeros((owners * slot_cap, feature_count), jnp.float32).at[slot_index]  13.1 us
  transfers between devices with their start and end apart: 3, of which 2 were waited for; matrix products, arithmetic and copies ran while one was open for 3% of the time, Pallas kernels for 0%

commit v1 on v0

--- a/solution.py
+++ b/solution.py
@@ -186,13 +186,20 @@
         onehot_rows, incoming[1], precision=EXACT_MATMUL
     )
     session_means = overall_sum / jnp.where(overall_count > 0.0, overall_count, 1.0)[:, None]
-    returned_means = lax.all_to_all(
-        session_means.reshape(owners, slot_cap, feature_count),
-        "users",
-        split_axis=0,
-        concat_axis=0,
-        tiled=True,
-    )
+    x = session_means.reshape(owners, slot_cap, feature_count)
+    ways, here = (lax.axis_size("users"), lax.axis_index("users"))
+    width = x.shape[0] // ways
+    shape = list(x.shape)
+    shape[0] = width
+    height = shape[0]
+    shape[0] = height * ways
+    full = jnp.zeros(shape, x.dtype)
+    for mask in range(ways):
+        part = lax.dynamic_slice_in_dim(x, (here ^ mask) * width, width, axis=0)
+        if mask:
+            part = lax.ppermute(part, "users", [(d, d ^ mask) for d in range(ways)])
+        full = lax.dynamic_update_slice_in_dim(full, part, (here ^ mask) * height, axis=0)
+    returned_means = full
     result = returned_means.reshape(owners * slot_cap, feature_count)[slot_index]
     return result
 

time: 387 us -> 381 us (0.984)
  the two profiles are of different devices: /device:TPU:0 before, /device:TPU:9 now
where the time goes in v1:
time: 381 us; the launch traced here: 380 us
  waiting for transfers between devices  173 us (45%)
  matrix products  85.9 us (23%)
  local copies, waits for them, and re-layouts  58.9 us (15%)
  starting transfers between devices  26.1 us (7%)
  blocking collectives  17.8 us (5%)
  other arithmetic  16.2 us (4%)
    all_to_all x1, waiting for transfers between devices, body(): lax.all_to_all(send_values.reshape(owners, slot_cap, feature_count), 'use...  90.2 us
    ppermute x7, waiting for transfers between devices, body(): part = lax.ppermute(part, 'users', [(d, d ^ mask) for d in range(ways)])  83 us
    dot_general x16, matrix products, session_advance(): inside_sum = jnp.dot(same_session, rows_values, precision=EXACT_MATMUL)  27.2 us
    dot_general x16, matrix products, session_advance(): jnp.dot(indicator_matrix, open_sum, precision=EXACT_MATMUL)  17.9 us
    gather x1, local copies, waits for them, and re-layouts, body(): returned_means.reshape(owners * slot_cap, feature_count)[slot_index]  16.4 us
    scatter x1, local copies, waits for them, and re-layouts, body(): jnp.full((owners * slot_cap,), -1.0, jnp.float32).at[slot_index]  16.1 us
    ppermute x7, starting transfers between devices, body(): part = lax.ppermute(part, 'users', [(d, d ^ mask) for d in range(ways)])  15.4 us
    dot_general x16, matrix products, session_advance(): jnp.dot(up_to_float, indicator_matrix * rows_flag[:, None], precision=EXA...  14.3 us
  transfers between devices with their start and end apart: 9, of which 6 were waited for; matrix products, arithmetic and copies ran while one was open for 5% of the time, Pallas kernels for 0%

profile of v1, /device:TPU:9, one launch (start us, length us, event | category | flops | bytes accessed | tf_op | source)
XLA Modules:
  0.0 379.6 jit_solution(17573109076530319233)
XLA Ops:
  0.6 1.4 reduce.7
  2.1 5.3 %while.34 = (s32[]{:T(128)}, f32[8]{0:T(128)S(1)}, f32[8,512]{1,0:T(8,128)S(1)}, s32[8,512]{1,0:T(8,128)S(1)}, s32[]{:T(128)}, /*index=5*/s32[]{:T(128)}) while((s32[]{:T(128)}, f32[8]{0:T(128)S(1)}, f32[8,512]{1,0:T(8,128)S(1)}, s32[8,512]{1,0:T(8,128)S(1)}, s32[]{:T(128)}, /*index=5*/s32[]{:T(128)}) %tuple.76), condition=%wide.region_3.4_spmd.clone, body=%wide.region_0.3_spmd.clone.sunk | while | flops 25722380 | bytes 14615 | solution.py:26
  8.9 16.1 %scatter_custom_fusion = f32[8192]{0:T(1024)} fusion(s32[4096]{0:T(1024)S(1)} %bitcast.171, f32[4096]{0:T(1024)S(1)} %add_convert_fusion, f32[]{:T(128)} %constant.53.clone.1), kind=kCustom, calls=%fused_computation.135 | custom fusion | bytes 32772 | tf_op jit(solution)/shard_map/scatter | solution.py:139
  25.0 5.6 %all-to-all-start = ((f32[8,1,1024]{2,1,0:T(1,128)}), f32[8,1,1024]{2,1,0:T(1,128)S(1)}, u32[]{:S(2)}, u32[]{:S(2)}) async-start(f32[8,1,1024]{2,1,0:T(1,128)} %bitcast.1), calls=%async_computation | async-start | bytes 65536 | tf_op jit(solution)/shard_map/all_to_all | solution.py:148
  30.6 13.1 %scatter_custom_fusion.1 = f32[8192,128]{1,0:T(8,128)} fusion(s32[4096]{0:T(1024)S(1)} %bitcast.172, f32[4096,128]{1,0:T(8,128)} %param.8, f32[]{:T(128)} %constant.46.clone.1), kind=kCustom, calls=%fused_computation.88 | custom fusion | bytes 4194816 | tf_op jit(solution)/shard_map/scatter | solution.py:137
  43.7 5.1 %all-to-all-start.1 = ((f32[8,1024,128]{2,1,0:T(8,128)}), f32[8,1024,128]{2,1,0:T(8,128)}, u32[]{:S(2)}, u32[]{:S(2)}) async-start(f32[8,1024,128]{2,1,0:T(8,128)} %bitcast.149), calls=%async_computation.1 | async-start | bytes 8388608 | tf_op jit(solution)/shard_map/all_to_all | solution.py:141
  49.1 90.2 %all-to-all-done.1 = f32[8,1024,128]{2,1,0:T(8,128)} async-done(((f32[8,1024,128]{2,1,0:T(8,128)}), f32[8,1024,128]{2,1,0:T(8,128)}, u32[]{:S(2)}, u32[]{:S(2)}) %all-to-all-start.1) | async-done | bytes 4194336 | tf_op jit(solution)/shard_map/all_to_all | solution.py:141
  139.3 90.2 %while.35 = (s32[]{:T(128)}, f32[128,128]{1,0:T(8,128)S(1)}, f32[128]{0:T(128)S(1)}, f32[128]{0:T(128)S(1)}, f32[16,512,128]{2,1,0:T(8,128)}, /*index=5*/f32[16,...) while((s32[]{:T(128)}, f32[128,128]{1,0:T(8,128)S(1)}, ...), condition=%wide.region_12.13_spmd.clone, body=%wide.region_6.12_spmd.clone.sunk | while | flops 1016011008 | bytes 1868948 | solution.py:111
  140.4 1.7 fusion.150
  146.0 1.7 fusion.150
  151.6 1.7 fusion.150
  157.3 1.7 fusion.150
  159.0 1.1 bitcast_dynamic-update-slice_fusion.2
  162.9 1.7 fusion.150
  168.6 1.7 fusion.150
  170.3 1.1 bitcast_dynamic-update-slice_fusion.2
  174.2 1.7 fusion.150
  179.9 1.7 fusion.150
  181.6 1.1 bitcast_dynamic-update-slice_fusion.2
  185.5 1.7 fusion.150
  191.2 1.7 fusion.150
  196.8 1.7 fusion.150
  198.5 1.1 bitcast_dynamic-update-slice_fusion.2
  202.5 1.7 fusion.150
  204.2 1.1 bitcast_dynamic-update-slice_fusion.2
  208.1 1.7 fusion.150
  213.7 1.7 fusion.150
  219.4 1.7 fusion.150
  225.0 1.7 fusion.150
  226.7 1.1 bitcast_dynamic-update-slice_fusion.2
  229.5 5.9 %all-gather = f32[4,1,128]{2,1,0:T(1,128)S(1)} all-gather(f32[1,1,128]{2,1,0:T(1,128)S(1)} %bitcast.182), channel_id=1, replica_groups=mesh['tm'=4,'users'=8] {'tm'}, dimensions={0}, use_global_device_ids=true | all-gather | bytes 2560 | tf_op jit(solution)/shard_map/all_gather | solution.py:164
  235.4 5.9 %all-gather.1 = f32[4,1,128]{2,1,0:T(1,128)S(1)} all-gather(f32[1,1,128]{2,1,0:T(1,128)S(1)} %bitcast.183), channel_id=1, replica_groups=mesh['tm'=4,'users'=8] {'tm'}, dimensions={0}, use_global_device_ids=true | all-gather | bytes 2560 | tf_op jit(solution)/shard_map/all_gather | solution.py:163
  241.3 6.0 %all_gather.9 = f32[512,128]{1,0:T(8,128)S(1)} all-gather(f32[128,128]{1,0:T(8,128)S(1)} %get-tuple-element.117), channel_id=1, replica_groups=mesh['tm'=4,'users'=8] {'tm'}, dimensions={0}, use_global_device_ids=true | all-gather | bytes 327680 | tf_op jit(solution)/shard_map/all_gather | solution.py:162
  247.3 2.9 fusion.58
  250.3 5.3 %fusion.57 = f32[8192,128]{1,0:T(8,128)S(1)} fusion(f32[8192,128]{1,0:T(8,128)} %bitcast.184, f32[8192]{0:T(1024)S(1)} %compare_select_fusion.1, s32[8192]{0:T(1024)S(1)} %fusion.78, f32[8192]{0:T(1024)S(1)} %bitcast.169, f32[512,128]{1,0:T(8,128)S(1)} %all_gather.9, f32[128]{0:T(128)S(1)} %get-tuple-element.240, f32[128]{0:T(128)S(1)} %get-tuple-element.238, ...), kind=kOutput, calls=%fused_computation.83 | convolution fusion | flops 1614987264 | bytes 8751108 | tf_op jit(solution)/shard_map/dot_general | solution.py:182
  255.6 2.3 broadcast_in_dim.55
  257.8 1.1 constant_dynamic-slice_fusion.3
  259.0 6.5 %collective-permute-start = (f32[1,1024,128]{2,1,0:T(8,128)S(1)}, f32[1,1024,128]{2,1,0:T(8,128)S(1)}, u32[]{:S(2)}, u32[]{:S(2)}) collective-permute-start(f32[1,1024,128]{2,1,0:T(8,128)S(1)} %get-tuple-element.233), channel_id=1, source_target_pairs={{0,1},{1,0},{2,3},{3,2},{4,5},{5,4},{6,7},{7,6},{8,9},{9,8},{10,11... | collective-permute-start | bytes 1572872 | tf_op jit(solution)/shard_map/ppermute | solution.py:200
  265.5 3.2 collective-permute-start.1
  268.7 1.5 collective-permute-start.3
  270.2 1.5 collective-permute-start.4
  272.7 26.9 %collective-permute-done.1 = f32[1,1024,128]{2,1,0:T(8,128)S(1)} collective-permute-done((f32[1,1024,128]{2,1,0:T(8,128)S(1)}, f32[1,1024,128]{2,1,0:T(8,128)S(1)}, u32[]{:S(2)}, u32[]{:S(2)}) %collective-permute-start.1) | collective-permute-done | bytes 524320 | tf_op jit(solution)/shard_map/ppermute | solution.py:200
  299.6 2.6 collective-permute-start.6
  303.0 7.8 %collective-permute-done.2 = f32[1,1024,128]{2,1,0:T(8,128)S(1)} collective-permute-done((f32[1,1024,128]{2,1,0:T(8,128)S(1)}, f32[1,1024,128]{2,1,0:T(8,128)S(1)}, u32[]{:S(2)}, u32[]{:S(2)}) %collective-permute-start.2) | collective-permute-done | bytes 524320 | tf_op jit(solution)/shard_map/ppermute | solution.py:200
  312.5 25.0 %collective-permute-done.4 = f32[1,1024,128]{2,1,0:T(8,128)S(1)} collective-permute-done((f32[1,1024,128]{2,1,0:T(8,128)S(1)}, f32[1,1024,128]{2,1,0:T(8,128)S(1)}, u32[]{:S(2)}, u32[]{:S(2)}) %collective-permute-start.4) | collective-permute-done | bytes 524320 | tf_op jit(solution)/shard_map/ppermute | solution.py:200
  338.3 12.5 %collective-permute-done.5 = f32[1,1024,128]{2,1,0:T(8,128)S(1)} collective-permute-done((f32[1,1024,128]{2,1,0:T(8,128)S(1)}, f32[1,1024,128]{2,1,0:T(8,128)S(1)}, u32[]{:S(2)}, u32[]{:S(2)}) %collective-permute-start.5) | collective-permute-done | bytes 524320 | tf_op jit(solution)/shard_map/ppermute | solution.py:200
  351.7 10.8 %collective-permute-done.6 = f32[1,1024,128]{2,1,0:T(8,128)S(1)} collective-permute-done((f32[1,1024,128]{2,1,0:T(8,128)S(1)}, f32[1,1024,128]{2,1,0:T(8,128)S(1)}, u32[]{:S(2)}, u32[]{:S(2)}) %collective-permute-start.6) | collective-permute-done | bytes 524320 | tf_op jit(solution)/shard_map/ppermute | solution.py:200
  363.3 16.4 %gather_fusion = f32[4096,128]{1,0:T(8,128)} fusion(f32[8192,128]{1,0:T(8,128)} %bitcast.19, s32[4096]{0:T(1024)S(1)} %broadcast_clamp_fusion), kind=kCustom, calls=%fused_computation | custom fusion | bytes 4210688 | tf_op jit(solution)/shard_map/gather | solution.py:203
  (310 shorter events, 68.6 us)
Async XLA Ops:
  25.0 18.7 %all-to-all-start = ((f32[8,1,1024]{2,1,0:T(1,128)}), f32[8,1,1024]{2,1,0:T(1,128)S(1)}, u32[]{:S(2)}, u32[]{:S(2)}) async-start(f32[8,1,1024]{2,1,0:T(1,128)} %bitcast.1), calls=%async_computation | async-start | bytes 65536 | tf_op jit(solution)/shard_map/all_to_all | solution.py:148
  43.7 95.6 %all-to-all-start.1 = ((f32[8,1024,128]{2,1,0:T(8,128)}), f32[8,1024,128]{2,1,0:T(8,128)}, u32[]{:S(2)}, u32[]{:S(2)}) async-start(f32[8,1024,128]{2,1,0:T(8,128)} %bitcast.149), calls=%async_computation.1 | async-start | bytes 8388608 | tf_op jit(solution)/shard_map/all_to_all | solution.py:141
  259.0 12.7 %collective-permute-start = (f32[1,1024,128]{2,1,0:T(8,128)S(1)}, f32[1,1024,128]{2,1,0:T(8,128)S(1)}, u32[]{:S(2)}, u32[]{:S(2)}) collective-permute-start(f32[1,1024,128]{2,1,0:T(8,128)S(1)} %get-tuple-element.233), channel_id=1, source_target_pairs={{0,1},{1,0},{2,3},{3,2},{4,5},{5,4},{6,7},{7,6},{8,9},{9,8},{10,11... | collective-permute-start | bytes 1572872 | tf_op jit(solution)/shard_map/ppermute | solution.py:200
  265.5 34.1 %collective-permute-start.1 = (f32[1,1024,128]{2,1,0:T(8,128)S(1)}, f32[1,1024,128]{2,1,0:T(8,128)S(1)}, u32[]{:S(2)}, u32[]{:S(2)}) collective-permute-start(f32[1,1024,128]{2,1,0:T(8,128)S(1)} %get-tuple-element.232), channel_id=1, source_target_pairs={{0,2},{1,3},{2,0},{3,1},{4,6},{5,7},{6,4},{7,5},{8,10},{9,11},{10,... | collective-permute-start | bytes 1572872 | tf_op jit(solution)/shard_map/ppermute | solution.py:200
  268.7 42.1 %collective-permute-start.2 = (f32[1,1024,128]{2,1,0:T(8,128)S(1)}, f32[1,1024,128]{2,1,0:T(8,128)S(1)}, u32[]{:S(2)}, u32[]{:S(2)}) collective-permute-start(f32[1,1024,128]{2,1,0:T(8,128)S(1)} %get-tuple-element.231), channel_id=1, source_target_pairs={{0,3},{1,2},{2,1},{3,0},{4,7},{5,6},{6,5},{7,4},{8,11},{9,10},{10,... | collective-permute-start | bytes 1572872 | tf_op jit(solution)/shard_map/ppermute | solution.py:200
  268.7 42.9 %collective-permute-start.3 = (f32[1,1024,128]{2,1,0:T(8,128)S(1)}, f32[1,1024,128]{2,1,0:T(8,128)S(1)}, u32[]{:S(2)}, u32[]{:S(2)}) collective-permute-start(f32[1,1024,128]{2,1,0:T(8,128)S(1)} %get-tuple-element.230), channel_id=1, source_target_pairs={{0,4},{1,5},{2,6},{3,7},{4,0},{5,1},{6,2},{7,3},{8,12},{9,13},{10,... | collective-permute-start | bytes 1572872 | tf_op jit(solution)/shard_map/ppermute | solution.py:200
  270.2 67.3 %collective-permute-start.4 = (f32[1,1024,128]{2,1,0:T(8,128)S(1)}, f32[1,1024,128]{2,1,0:T(8,128)S(1)}, u32[]{:S(2)}, u32[]{:S(2)}) collective-permute-start(f32[1,1024,128]{2,1,0:T(8,128)S(1)} %get-tuple-element.229), channel_id=1, source_target_pairs={{0,5},{1,4},{2,7},{3,6},{4,1},{5,0},{6,3},{7,2},{8,13},{9,12},{10,... | collective-permute-start | bytes 1572872 | tf_op jit(solution)/shard_map/ppermute | solution.py:200
  271.7 79.1 %collective-permute-start.5 = (f32[1,1024,128]{2,1,0:T(8,128)S(1)}, f32[1,1024,128]{2,1,0:T(8,128)S(1)}, u32[]{:S(2)}, u32[]{:S(2)}) collective-permute-start(f32[1,1024,128]{2,1,0:T(8,128)S(1)} %get-tuple-element.228), channel_id=1, source_target_pairs={{0,6},{1,7},{2,4},{3,5},{4,2},{5,3},{6,0},{7,1},{8,14},{9,15},{10,... | collective-permute-start | bytes 1572872 | tf_op jit(solution)/shard_map/ppermute | solution.py:200
  299.6 62.9 %collective-permute-start.6 = (f32[1,1024,128]{2,1,0:T(8,128)S(1)}, f32[1,1024,128]{2,1,0:T(8,128)S(1)}, u32[]{:S(2)}, u32[]{:S(2)}) collective-permute-start(f32[1,1024,128]{2,1,0:T(8,128)S(1)} %get-tuple-element.227), channel_id=1, source_target_pairs={{0,7},{1,6},{2,5},{3,4},{4,3},{5,2},{6,1},{7,0},{8,15},{9,14},{10,... | collective-permute-start | bytes 1572872 | tf_op jit(solution)/shard_map/ppermute | solution.py:200
